TPU v7x, 32 devices: a whole 2x2x4 slice. The times are simulated.
32 devices in a mesh: ia: 4 (over y, x), ja: 4 (over z), ka: 2 (over core).
Axes of the slice: x: 2, y: 2, z: 4, core: 2. Of those that a mesh axis runs over, the one named last changes fastest.
Arguments:
- tensor: bfloat16 [1024, 512, 256], P('ia', 'ja', 'ka'), may hold values from -6 to 6
- factor_b: bfloat16 [512, 256], P('ja', 'ka'), may hold values from -16 to 16
- factor_c: bfloat16 [256, 256], P('ka', 'ja'), may hold values from -16 to 16
Outputs:
- factor_a: float32 [1024, 256], P(('ia', 'ja', 'ka'))
All inputs are finite; a program needn't handle non-finite values.
Results may differ from a plain program's by a relative error of at most 0.0003.
Values may be sent and summed in bfloat16 or wider, within the bound.
No kernel may reach another device: no remote copies, remote signals or barrier semaphores. Data moves between devices by JAX's collectives and lax.ppermute only.
A program may use at most 64 MiB of HBM per device.

v0:
```python
import math
import jax
import jax.numpy as jnp
from jax import lax
from jax.sharding import PartitionSpec as P

ridge_weight = 0.1


def contract(block, b_wide, c_wide):
    rows, width_j, width_k = block.shape
    inner = jnp.dot(
        block.reshape(rows * width_j, width_k), c_wide, preferred_element_type=jnp.float32
    )
    inner = inner.reshape(rows, width_j, -1)
    return jnp.sum(inner * b_wide.astype(jnp.float32)[None], axis=1)


def partial_rows(tensor, b_wide, c_wide, row_count):
    step_rows = math.gcd(row_count, 16)
    pieces = tensor.reshape(row_count // step_rows, step_rows, tensor.shape[1], tensor.shape[2])
    result = lax.map(lambda piece: contract(piece, b_wide, c_wide), pieces)
    return result.reshape(row_count, b_wide.shape[1])


def body(tensor, factor_b, factor_c):
    b_wide = lax.all_gather(factor_b, "ka", axis=1, tiled=True)
    c_wide = lax.all_gather(factor_c, "ja", axis=1, tiled=True)
    rank = b_wide.shape[1]
    gram_b = lax.psum(jnp.dot(b_wide.T, b_wide, preferred_element_type=jnp.float32), "ja")
    gram_c = lax.psum(jnp.dot(c_wide.T, c_wide, preferred_element_type=jnp.float32), "ka")
    normal_matrix = gram_b * gram_c + ridge_weight * jnp.eye(rank, dtype=jnp.float32)
    block_rows = tensor.shape[0]
    owned = block_rows // (lax.axis_size("ja") * lax.axis_size("ka"))
    mine = lax.psum_scatter(
        partial_rows(tensor, b_wide, c_wide, owned * lax.axis_size(("ja", "ka"))),
        ("ja", "ka"),
        scatter_dimension=0,
        tiled=True,
    )
    lower = jnp.linalg.cholesky(normal_matrix)
    solved = jax.scipy.linalg.cho_solve((lower, True), mine.T)
    return solved.T


def solution(mesh):
    placed = (P("ia", "ja", "ka"), P("ja", "ka"), P("ka", "ja"))
    return jax.shard_map(
        body, mesh=mesh, in_specs=placed, out_specs=P(("ia", "ja", "ka"), None), check_vma=False
    )
```

profile of v0, /device:TPU:0, one launch (start us, length us, event | category | flops | bytes accessed | tf_op | source)
XLA Modules:
  0.0 142.1 jit_solution(7812872350361288820)
XLA Ops:
  7.4 2.2 %all_gather.6 = bf16[128,256]{1,0:T(8,128)(2,1)S(1)} all-gather(bf16[128,128]{1,0:T(8,128)(2,1)} %param.6), channel_id=1, replica_groups=mesh['ia'=4,'ja'=4,'ka'=2] {'ka'}, dimensions={1}, use_global_device_ids=true | all-gather | bytes 98304 | tf_op jit(solution)/shard_map/all_gather | solution.py:27
  9.6 0.9 fusion.16
  10.6 15.2 %all_gather.7 = bf16[128,256]{0,1:T(8,128)(2,1)S(1)} all-gather(bf16[128,64]{0,1:T(8,128)(2,1)} %param.7), channel_id=1, replica_groups=mesh['ia'=4,'ja'=4,'ka'=2] {'ja'}, dimensions={1}, use_global_device_ids=true | all-gather | bytes 81920 | tf_op jit(solution)/shard_map/all_gather | solution.py:28
  25.8 0.9 fusion.17
  26.9 33.7 %while.11 = (s32[]{:T(128)}, f32[16,16,256]{2,1,0:T(8,128)}, bf16[16,16,128,128]{3,2,1,0:T(8,128)(2,1)}, bf16[128,256]{1,0:T(8,128)(2,1)S(1)}, bf16[128,256]{1,0:T(8,128)(2,1)S(1)}, /*index=5*/s32[]{:T(128)}) while((s32[]{:T(128)}, f32[16,16,256]{2,1,0:T(8,128)}, bf16[16,16,128,128]{3,2,1,0:T(8,128)(2,1)}, bf16[128,256]{1,0:T(8,128)(2,1)S(1)}, ...), condition=%wide.region_8.9_spmd, body=%wide.region_6.8_spmd.sunk | while | flops 135294976 | bytes 967749 | solution.py:22
  26.9 1.5 %multiply_reduce_fusion.2 = f32[16,256]{1,0:T(8,128)S(1)} fusion(f32[128,256]{1,0:T(8,128)S(1)} %convert_element_type.9, bf16[16,16,128,128]{3,2,1,0:T(8,128)(2,1)} %get-tuple-element.167, s32[]{:T(128)} %get-tuple-element.159, bf16[128,256]{1,0:T(8,128)(2,1)S(1)} %get-tuple-element.168), kind=kOutput, calls=%fused_computation.clone.1 | convolution fusion | flops 135262208 | bytes 737792 | tf_op jit(solution)/shard_map/while/body/eval_jaxpr/dot_general | solution.py:12
  28.4 0.6 bitcast_dynamic-update-slice_fusion.4
  29.0 1.5 %multiply_reduce_fusion.2 = f32[16,256]{1,0:T(8,128)S(1)} fusion(f32[128,256]{1,0:T(8,128)S(1)} %convert_element_type.9, bf16[16,16,128,128]{3,2,1,0:T(8,128)(2,1)} %get-tuple-element.167, s32[]{:T(128)} %get-tuple-element.159, bf16[128,256]{1,0:T(8,128)(2,1)S(1)} %get-tuple-element.168), kind=kOutput, calls=%fused_computation.clone.1 | convolution fusion | flops 135262208 | bytes 737792 | tf_op jit(solution)/shard_map/while/body/eval_jaxpr/dot_general | solution.py:12
  31.1 1.5 %multiply_reduce_fusion.2 = f32[16,256]{1,0:T(8,128)S(1)} fusion(f32[128,256]{1,0:T(8,128)S(1)} %convert_element_type.9, bf16[16,16,128,128]{3,2,1,0:T(8,128)(2,1)} %get-tuple-element.167, s32[]{:T(128)} %get-tuple-element.159, bf16[128,256]{1,0:T(8,128)(2,1)S(1)} %get-tuple-element.168), kind=kOutput, calls=%fused_computation.clone.1 | convolution fusion | flops 135262208 | bytes 737792 | tf_op jit(solution)/shard_map/while/body/eval_jaxpr/dot_general | solution.py:12
  32.6 0.6 bitcast_dynamic-update-slice_fusion.4
  33.2 1.5 %multiply_reduce_fusion.2 = f32[16,256]{1,0:T(8,128)S(1)} fusion(f32[128,256]{1,0:T(8,128)S(1)} %convert_element_type.9, bf16[16,16,128,128]{3,2,1,0:T(8,128)(2,1)} %get-tuple-element.167, s32[]{:T(128)} %get-tuple-element.159, bf16[128,256]{1,0:T(8,128)(2,1)S(1)} %get-tuple-element.168), kind=kOutput, calls=%fused_computation.clone.1 | convolution fusion | flops 135262208 | bytes 737792 | tf_op jit(solution)/shard_map/while/body/eval_jaxpr/dot_general | solution.py:12
  34.7 0.6 bitcast_dynamic-update-slice_fusion.4
  35.3 1.5 %multiply_reduce_fusion.2 = f32[16,256]{1,0:T(8,128)S(1)} fusion(f32[128,256]{1,0:T(8,128)S(1)} %convert_element_type.9, bf16[16,16,128,128]{3,2,1,0:T(8,128)(2,1)} %get-tuple-element.167, s32[]{:T(128)} %get-tuple-element.159, bf16[128,256]{1,0:T(8,128)(2,1)S(1)} %get-tuple-element.168), kind=kOutput, calls=%fused_computation.clone.1 | convolution fusion | flops 135262208 | bytes 737792 | tf_op jit(solution)/shard_map/while/body/eval_jaxpr/dot_general | solution.py:12
  36.8 0.6 bitcast_dynamic-update-slice_fusion.4
  37.4 1.5 %multiply_reduce_fusion.2 = f32[16,256]{1,0:T(8,128)S(1)} fusion(f32[128,256]{1,0:T(8,128)S(1)} %convert_element_type.9, bf16[16,16,128,128]{3,2,1,0:T(8,128)(2,1)} %get-tuple-element.167, s32[]{:T(128)} %get-tuple-element.159, bf16[128,256]{1,0:T(8,128)(2,1)S(1)} %get-tuple-element.168), kind=kOutput, calls=%fused_computation.clone.1 | convolution fusion | flops 135262208 | bytes 737792 | tf_op jit(solution)/shard_map/while/body/eval_jaxpr/dot_general | solution.py:12
  39.5 1.5 %multiply_reduce_fusion.2 = f32[16,256]{1,0:T(8,128)S(1)} fusion(f32[128,256]{1,0:T(8,128)S(1)} %convert_element_type.9, bf16[16,16,128,128]{3,2,1,0:T(8,128)(2,1)} %get-tuple-element.167, s32[]{:T(128)} %get-tuple-element.159, bf16[128,256]{1,0:T(8,128)(2,1)S(1)} %get-tuple-element.168), kind=kOutput, calls=%fused_computation.clone.1 | convolution fusion | flops 135262208 | bytes 737792 | tf_op jit(solution)/shard_map/while/body/eval_jaxpr/dot_general | solution.py:12
  41.0 0.6 bitcast_dynamic-update-slice_fusion.4
  41.6 1.5 %multiply_reduce_fusion.2 = f32[16,256]{1,0:T(8,128)S(1)} fusion(f32[128,256]{1,0:T(8,128)S(1)} %convert_element_type.9, bf16[16,16,128,128]{3,2,1,0:T(8,128)(2,1)} %get-tuple-element.167, s32[]{:T(128)} %get-tuple-element.159, bf16[128,256]{1,0:T(8,128)(2,1)S(1)} %get-tuple-element.168), kind=kOutput, calls=%fused_computation.clone.1 | convolution fusion | flops 135262208 | bytes 737792 | tf_op jit(solution)/shard_map/while/body/eval_jaxpr/dot_general | solution.py:12
  43.1 0.6 bitcast_dynamic-update-slice_fusion.4
  43.7 1.5 %multiply_reduce_fusion.2 = f32[16,256]{1,0:T(8,128)S(1)} fusion(f32[128,256]{1,0:T(8,128)S(1)} %convert_element_type.9, bf16[16,16,128,128]{3,2,1,0:T(8,128)(2,1)} %get-tuple-element.167, s32[]{:T(128)} %get-tuple-element.159, bf16[128,256]{1,0:T(8,128)(2,1)S(1)} %get-tuple-element.168), kind=kOutput, calls=%fused_computation.clone.1 | convolution fusion | flops 135262208 | bytes 737792 | tf_op jit(solution)/shard_map/while/body/eval_jaxpr/dot_general | solution.py:12
  45.2 0.6 bitcast_dynamic-update-slice_fusion.4
  45.8 1.5 %multiply_reduce_fusion.2 = f32[16,256]{1,0:T(8,128)S(1)} fusion(f32[128,256]{1,0:T(8,128)S(1)} %convert_element_type.9, bf16[16,16,128,128]{3,2,1,0:T(8,128)(2,1)} %get-tuple-element.167, s32[]{:T(128)} %get-tuple-element.159, bf16[128,256]{1,0:T(8,128)(2,1)S(1)} %get-tuple-element.168), kind=kOutput, calls=%fused_computation.clone.1 | convolution fusion | flops 135262208 | bytes 737792 | tf_op jit(solution)/shard_map/while/body/eval_jaxpr/dot_general | solution.py:12
  47.9 1.5 %multiply_reduce_fusion.2 = f32[16,256]{1,0:T(8,128)S(1)} fusion(f32[128,256]{1,0:T(8,128)S(1)} %convert_element_type.9, bf16[16,16,128,128]{3,2,1,0:T(8,128)(2,1)} %get-tuple-element.167, s32[]{:T(128)} %get-tuple-element.159, bf16[128,256]{1,0:T(8,128)(2,1)S(1)} %get-tuple-element.168), kind=kOutput, calls=%fused_computation.clone.1 | convolution fusion | flops 135262208 | bytes 737792 | tf_op jit(solution)/shard_map/while/body/eval_jaxpr/dot_general | solution.py:12
  49.4 0.6 bitcast_dynamic-update-slice_fusion.4
  50.0 1.5 %multiply_reduce_fusion.2 = f32[16,256]{1,0:T(8,128)S(1)} fusion(f32[128,256]{1,0:T(8,128)S(1)} %convert_element_type.9, bf16[16,16,128,128]{3,2,1,0:T(8,128)(2,1)} %get-tuple-element.167, s32[]{:T(128)} %get-tuple-element.159, bf16[128,256]{1,0:T(8,128)(2,1)S(1)} %get-tuple-element.168), kind=kOutput, calls=%fused_computation.clone.1 | convolution fusion | flops 135262208 | bytes 737792 | tf_op jit(solution)/shard_map/while/body/eval_jaxpr/dot_general | solution.py:12
  51.5 0.6 bitcast_dynamic-update-slice_fusion.4
  52.1 1.5 %multiply_reduce_fusion.2 = f32[16,256]{1,0:T(8,128)S(1)} fusion(f32[128,256]{1,0:T(8,128)S(1)} %convert_element_type.9, bf16[16,16,128,128]{3,2,1,0:T(8,128)(2,1)} %get-tuple-element.167, s32[]{:T(128)} %get-tuple-element.159, bf16[128,256]{1,0:T(8,128)(2,1)S(1)} %get-tuple-element.168), kind=kOutput, calls=%fused_computation.clone.1 | convolution fusion | flops 135262208 | bytes 737792 | tf_op jit(solution)/shard_map/while/body/eval_jaxpr/dot_general | solution.py:12
  53.6 0.6 bitcast_dynamic-update-slice_fusion.4
  54.2 1.5 %multiply_reduce_fusion.2 = f32[16,256]{1,0:T(8,128)S(1)} fusion(f32[128,256]{1,0:T(8,128)S(1)} %convert_element_type.9, bf16[16,16,128,128]{3,2,1,0:T(8,128)(2,1)} %get-tuple-element.167, s32[]{:T(128)} %get-tuple-element.159, bf16[128,256]{1,0:T(8,128)(2,1)S(1)} %get-tuple-element.168), kind=kOutput, calls=%fused_computation.clone.1 | convolution fusion | flops 135262208 | bytes 737792 | tf_op jit(solution)/shard_map/while/body/eval_jaxpr/dot_general | solution.py:12
  56.3 1.5 %multiply_reduce_fusion.2 = f32[16,256]{1,0:T(8,128)S(1)} fusion(f32[128,256]{1,0:T(8,128)S(1)} %convert_element_type.9, bf16[16,16,128,128]{3,2,1,0:T(8,128)(2,1)} %get-tuple-element.167, s32[]{:T(128)} %get-tuple-element.159, bf16[128,256]{1,0:T(8,128)(2,1)S(1)} %get-tuple-element.168), kind=kOutput, calls=%fused_computation.clone.1 | convolution fusion | flops 135262208 | bytes 737792 | tf_op jit(solution)/shard_map/while/body/eval_jaxpr/dot_general | solution.py:12
  57.8 0.6 bitcast_dynamic-update-slice_fusion.4
  58.4 1.5 %multiply_reduce_fusion.2 = f32[16,256]{1,0:T(8,128)S(1)} fusion(f32[128,256]{1,0:T(8,128)S(1)} %convert_element_type.9, bf16[16,16,128,128]{3,2,1,0:T(8,128)(2,1)} %get-tuple-element.167, s32[]{:T(128)} %get-tuple-element.159, bf16[128,256]{1,0:T(8,128)(2,1)S(1)} %get-tuple-element.168), kind=kOutput, calls=%fused_computation.clone.1 | convolution fusion | flops 135262208 | bytes 737792 | tf_op jit(solution)/shard_map/while/body/eval_jaxpr/dot_general | solution.py:12
  59.9 0.6 bitcast_dynamic-update-slice_fusion.4
  60.6 8.9 %all-reduce.6.cloned.1.call-done = f32[256,256]{0,1:T(8,128)} async-done(((f32[256,256]{0,1:T(8,128)}), f32[256,256]{0,1:T(8,128)}) %all-reduce.6.cloned.1.call-update) | async-done | bytes 262160 | tf_op jit(solution)/shard_map/psum | solution.py:31
  69.5 1.1 select_add_fusion
  70.8 11.7 %cholesky.49 = f32[128,128]{1,0:T(8,128)S(1)} custom-call(f32[128,128]{1,0:T(8,128)S(1)} %cholesky.115), custom_call_target="Cholesky" | custom-call | tf_op jit(solution)/shard_map/jit(cholesky)/cholesky | solution.py:41
  82.5 9.8 %custom-call.18 = f32[1,128,128]{1,2,0:T(8,128)S(1)} custom-call(f32[1,128,128]{2,1,0:T(8,128)S(1)} %get-tuple-element.75), custom_call_target="InvertDiagBlocksLowerTriangular" | custom-call | tf_op jit(solution)/shard_map/jit(cholesky)/cholesky | solution.py:41
  92.8 11.7 %cholesky.103 = f32[128,128]{1,0:T(8,128)S(1)} custom-call(f32[128,128]{1,0:T(8,128)S(1)} %convolution_subtract_fusion), custom_call_target="Cholesky" | custom-call | tf_op jit(solution)/shard_map/jit(cholesky)/cholesky | solution.py:41
  104.9 0.7 compare_reduce_fusion
  107.0 4.3 %while.12 = (s32[]{:T(128)}, f32[256,256]{0,1:T(8,128)S(1)}, s32[2,2]{1,0:T(2,128)S(1)}, f32[2,128,128]{2,1,0:T(8,128)S(1)}, s32[]{:T(128)}) while((s32[]{:T(128)}, f32[256,256]{0,1:T(8,128)S(1)}, s32[2,2]{1,0:T(2,128)S(1)}, f32[2,128,128]{2,1,0:T(8,128)S(1)}, s32[]{:T(128)}) %tuple.37), condition=%wide.while_cond, body=%wide.while_body.sunk | while | flops 2 | bytes 393321 | solution.py:42
  107.0 0.7 fusion.34
  107.7 1.3 dynamic-slice.7
  109.2 0.7 fusion.34
  109.9 1.3 dynamic-slice.7
  111.3 19.9 %custom-call.19 = f32[2,128,128]{1,2,0:T(8,128)S(1)} custom-call(f32[2,128,128]{2,1,0:T(8,128)S(1)} %get-tuple-element.40), custom_call_target="InvertDiagBlocksLowerTriangular" | custom-call | tf_op jit(solution)/shard_map/jit(_cho_solve)/triangular_solve | solution.py:42
  131.2 0.9 fusion.9
  132.1 0.9 convolution_subtract_fusion.2
  134.0 0.6 maximum_bitcast_fusion
  (57 shorter events, 5.2 us)
Async XLA Ops:
  7.4 53.2 %all-reduce.4.cloned.1.call-start = ((), (), s32[]{:S(2)}) async-start(), calls=%async_computation.1 | async-start | bytes 524288 | tf_op jit(solution)/shard_map/psum | solution.py:30
  10.5 59.0 %all-reduce.6.cloned.1.call-start = ((), (), s32[]{:S(2)}) async-start(), calls=%async_computation.2 | async-start | bytes 524288 | tf_op jit(solution)/shard_map/psum | solution.py:31
  26.7 104.5 %reduce-scatter.2.cloned.1.call-start = ((), (), s32[]{:S(2)}) async-start(), calls=%async_computation.3 | async-start | bytes 294912 | tf_op jit(solution)/shard_map/reduce_scatter | solution.py:35
Sparse Core Ops, SparseCore 0:
  10.7 38.3 all-reduce.3
  51.4 18.0 all-reduce.5
Sparse Core Ops, SparseCore 1:
  60.6 31.9 reduce-scatter.1
where the time goes:
time: 143 us; the launch traced here: 142 us
  other arithmetic  55.8 us (39%)
  matrix products  28.6 us (20%)
  blocking collectives  17.4 us (12%)
  between operations  16.3 us (11%)
  local copies, waits for them, and re-layouts  14.6 us (10%)
  waiting for transfers between devices  9.01 us (6%)
    another operation x6, other arithmetic, body(): lower = jnp.linalg.cholesky(normal_matrix)  34 us
    dot_general x16, matrix products, contract(): jnp.dot(block.reshape(rows * width_j, width_k), c_wide, preferred_element...  23.6 us
    another operation x3, other arithmetic, body(): solved = jax.scipy.linalg.cho_solve((lower, True), mine.T)  19.9 us
    all_gather x1, blocking collectives, body(): c_wide = lax.all_gather(factor_c, 'ja', axis=1, tiled=True)  15.2 us
    dynamic_update_slice x16, local copies, waits for them, and re-layouts, partial_rows(): result = lax.map(lambda piece: contract(piece, b_wide, c_wide), pieces)  9.71 us
    psum x1, waiting for transfers between devices, body(): lax.psum(jnp.dot(c_wide.T, c_wide, preferred_element_type=jnp.float32), '...  8.92 us
    another operation x10, local copies, waits for them, and re-layouts  4.22 us
  transfers between devices with their start and end apart: 3, of which 1 were waited for; matrix products, arithmetic and copies ran while one was open for 67% of the time, Pallas kernels for 0%

commit v1 on v0

--- a/solution.py
+++ b/solution.py
@@ -28,7 +28,9 @@
     c_wide = lax.all_gather(factor_c, "ja", axis=1, tiled=True)
     rank = b_wide.shape[1]
     gram_b = lax.psum(jnp.dot(b_wide.T, b_wide, preferred_element_type=jnp.float32), "ja")
-    gram_c = lax.psum(jnp.dot(c_wide.T, c_wide, preferred_element_type=jnp.float32), "ka")
+    gram_c = jnp.sum(
+        lax.all_gather(jnp.dot(c_wide.T, c_wide, preferred_element_type=jnp.float32), "ka"), axis=0
+    )
     normal_matrix = gram_b * gram_c + ridge_weight * jnp.eye(rank, dtype=jnp.float32)
     block_rows = tensor.shape[0]
     owned = block_rows // (lax.axis_size("ja") * lax.axis_size("ka"))

time: 143 us -> 136 us (0.951)
  waiting for transfers between devices: 9.01 us -> 0.08 us
  blocking collectives: 17.4 us -> 19.6 us
    psum x1 -> x0, waiting for transfers between devices: 8.92 us -> none  [body(): lax.psum(jnp.dot(c_wide.T, c_wide, preferred_element_type=jnp.float32), '...]
    all_gather x0 -> x1, blocking collectives: none -> 2.18 us  [body(): lax.all_gather(jnp.dot(c_wide.T, c_wide, preferred_element_type=jnp.float...]
  transfers between devices with their start and end apart: 3 -> 2, of which waited for: 1 -> 0; matrix products, arithmetic and copies ran while one was open for 67% -> 70% of each run, Pallas kernels for 0% -> 0%
where the time goes in v1:
time: 136 us; the launch traced here: 135 us
  other arithmetic  55.6 us (41%)
  matrix products  27.8 us (20%)
  blocking collectives  19.6 us (14%)
  between operations  16.3 us (12%)
  local copies, waits for them, and re-layouts  14.7 us (11%)
    another operation x6, other arithmetic, body(): lower = jnp.linalg.cholesky(normal_matrix)  34 us
    dot_general x16, matrix products, contract(): jnp.dot(block.reshape(rows * width_j, width_k), c_wide, preferred_element...  23.5 us
    another operation x3, other arithmetic, body(): solved = jax.scipy.linalg.cho_solve((lower, True), mine.T)  19.7 us
    all_gather x1, blocking collectives, body(): c_wide = lax.all_gather(factor_c, 'ja', axis=1, tiled=True)  15.2 us
    dynamic_update_slice x16, local copies, waits for them, and re-layouts, partial_rows(): result = lax.map(lambda piece: contract(piece, b_wide, c_wide), pieces)  9.69 us
    another operation x10, local copies, waits for them, and re-layouts  4.22 us
  transfers between devices with their start and end apart: 2, of which 0 were waited for; matrix products, arithmetic and copies ran while one was open for 70% of the time, Pallas kernels for 0%

profile of v1, /device:TPU:0, one launch (start us, length us, event | category | flops | bytes accessed | tf_op | source)
XLA Modules:
  0.0 134.5 jit_solution(1415388810884983687)
XLA Ops:
  7.4 2.2 %all_gather.12 = bf16[128,256]{1,0:T(8,128)(2,1)S(1)} all-gather(bf16[128,128]{1,0:T(8,128)(2,1)} %param.6), channel_id=1, replica_groups=mesh['ia'=4,'ja'=4,'ka'=2] {'ka'}, dimensions={1}, use_global_device_ids=true | all-gather | bytes 98304 | tf_op jit(solution)/shard_map/all_gather | solution.py:27
  9.6 0.9 fusion.16
  10.6 15.2 %all_gather.13 = bf16[128,256]{0,1:T(8,128)(2,1)S(1)} all-gather(bf16[128,64]{0,1:T(8,128)(2,1)} %param.7), channel_id=1, replica_groups=mesh['ia'=4,'ja'=4,'ka'=2] {'ja'}, dimensions={1}, use_global_device_ids=true | all-gather | bytes 81920 | tf_op jit(solution)/shard_map/all_gather | solution.py:28
  25.9 33.6 %while.11 = (s32[]{:T(128)}, f32[16,16,256]{2,1,0:T(8,128)}, bf16[16,16,128,128]{3,2,1,0:T(8,128)(2,1)}, bf16[128,256]{1,0:T(8,128)(2,1)S(1)}, bf16[128,256]{1,0:T(8,128)(2,1)S(1)}, /*index=5*/s32[]{:T(128)}) while((s32[]{:T(128)}, f32[16,16,256]{2,1,0:T(8,128)}, bf16[16,16,128,128]{3,2,1,0:T(8,128)(2,1)}, bf16[128,256]{1,0:T(8,128)(2,1)S(1)}, ...), condition=%wide.region_8.9_spmd, body=%wide.region_6.8_spmd.sunk | while | flops 135294976 | bytes 967749 | solution.py:22
  25.9 1.5 %multiply_reduce_fusion.2 = f32[16,256]{1,0:T(8,128)S(1)} fusion(f32[128,256]{1,0:T(8,128)S(1)} %convert_element_type.9, bf16[16,16,128,128]{3,2,1,0:T(8,128)(2,1)} %get-tuple-element.167, s32[]{:T(128)} %get-tuple-element.159, bf16[128,256]{1,0:T(8,128)(2,1)S(1)} %get-tuple-element.168), kind=kOutput, calls=%fused_computation.clone.1 | convolution fusion | flops 135262208 | bytes 737792 | tf_op jit(solution)/shard_map/while/body/eval_jaxpr/dot_general | solution.py:12
  27.4 0.6 bitcast_dynamic-update-slice_fusion.4
  28.0 1.5 %multiply_reduce_fusion.2 = f32[16,256]{1,0:T(8,128)S(1)} fusion(f32[128,256]{1,0:T(8,128)S(1)} %convert_element_type.9, bf16[16,16,128,128]{3,2,1,0:T(8,128)(2,1)} %get-tuple-element.167, s32[]{:T(128)} %get-tuple-element.159, bf16[128,256]{1,0:T(8,128)(2,1)S(1)} %get-tuple-element.168), kind=kOutput, calls=%fused_computation.clone.1 | convolution fusion | flops 135262208 | bytes 737792 | tf_op jit(solution)/shard_map/while/body/eval_jaxpr/dot_general | solution.py:12
  29.5 0.6 bitcast_dynamic-update-slice_fusion.4
  30.1 1.5 %multiply_reduce_fusion.2 = f32[16,256]{1,0:T(8,128)S(1)} fusion(f32[128,256]{1,0:T(8,128)S(1)} %convert_element_type.9, bf16[16,16,128,128]{3,2,1,0:T(8,128)(2,1)} %get-tuple-element.167, s32[]{:T(128)} %get-tuple-element.159, bf16[128,256]{1,0:T(8,128)(2,1)S(1)} %get-tuple-element.168), kind=kOutput, calls=%fused_computation.clone.1 | convolution fusion | flops 135262208 | bytes 737792 | tf_op jit(solution)/shard_map/while/body/eval_jaxpr/dot_general | solution.py:12
  31.6 0.6 bitcast_dynamic-update-slice_fusion.4
  32.2 1.5 %multiply_reduce_fusion.2 = f32[16,256]{1,0:T(8,128)S(1)} fusion(f32[128,256]{1,0:T(8,128)S(1)} %convert_element_type.9, bf16[16,16,128,128]{3,2,1,0:T(8,128)(2,1)} %get-tuple-element.167, s32[]{:T(128)} %get-tuple-element.159, bf16[128,256]{1,0:T(8,128)(2,1)S(1)} %get-tuple-element.168), kind=kOutput, calls=%fused_computation.clone.1 | convolution fusion | flops 135262208 | bytes 737792 | tf_op jit(solution)/shard_map/while/body/eval_jaxpr/dot_general | solution.py:12
  33.7 0.6 bitcast_dynamic-update-slice_fusion.4
  34.3 1.5 %multiply_reduce_fusion.2 = f32[16,256]{1,0:T(8,128)S(1)} fusion(f32[128,256]{1,0:T(8,128)S(1)} %convert_element_type.9, bf16[16,16,128,128]{3,2,1,0:T(8,128)(2,1)} %get-tuple-element.167, s32[]{:T(128)} %get-tuple-element.159, bf16[128,256]{1,0:T(8,128)(2,1)S(1)} %get-tuple-element.168), kind=kOutput, calls=%fused_computation.clone.1 | convolution fusion | flops 135262208 | bytes 737792 | tf_op jit(solution)/shard_map/while/body/eval_jaxpr/dot_general | solution.py:12
  36.4 1.5 %multiply_reduce_fusion.2 = f32[16,256]{1,0:T(8,128)S(1)} fusion(f32[128,256]{1,0:T(8,128)S(1)} %convert_element_type.9, bf16[16,16,128,128]{3,2,1,0:T(8,128)(2,1)} %get-tuple-element.167, s32[]{:T(128)} %get-tuple-element.159, bf16[128,256]{1,0:T(8,128)(2,1)S(1)} %get-tuple-element.168), kind=kOutput, calls=%fused_computation.clone.1 | convolution fusion | flops 135262208 | bytes 737792 | tf_op jit(solution)/shard_map/while/body/eval_jaxpr/dot_general | solution.py:12
  37.9 0.6 bitcast_dynamic-update-slice_fusion.4
  38.5 1.5 %multiply_reduce_fusion.2 = f32[16,256]{1,0:T(8,128)S(1)} fusion(f32[128,256]{1,0:T(8,128)S(1)} %convert_element_type.9, bf16[16,16,128,128]{3,2,1,0:T(8,128)(2,1)} %get-tuple-element.167, s32[]{:T(128)} %get-tuple-element.159, bf16[128,256]{1,0:T(8,128)(2,1)S(1)} %get-tuple-element.168), kind=kOutput, calls=%fused_computation.clone.1 | convolution fusion | flops 135262208 | bytes 737792 | tf_op jit(solution)/shard_map/while/body/eval_jaxpr/dot_general | solution.py:12
  40.0 0.6 bitcast_dynamic-update-slice_fusion.4
  40.6 1.5 %multiply_reduce_fusion.2 = f32[16,256]{1,0:T(8,128)S(1)} fusion(f32[128,256]{1,0:T(8,128)S(1)} %convert_element_type.9, bf16[16,16,128,128]{3,2,1,0:T(8,128)(2,1)} %get-tuple-element.167, s32[]{:T(128)} %get-tuple-element.159, bf16[128,256]{1,0:T(8,128)(2,1)S(1)} %get-tuple-element.168), kind=kOutput, calls=%fused_computation.clone.1 | convolution fusion | flops 135262208 | bytes 737792 | tf_op jit(solution)/shard_map/while/body/eval_jaxpr/dot_general | solution.py:12
  42.7 1.5 %multiply_reduce_fusion.2 = f32[16,256]{1,0:T(8,128)S(1)} fusion(f32[128,256]{1,0:T(8,128)S(1)} %convert_element_type.9, bf16[16,16,128,128]{3,2,1,0:T(8,128)(2,1)} %get-tuple-element.167, s32[]{:T(128)} %get-tuple-element.159, bf16[128,256]{1,0:T(8,128)(2,1)S(1)} %get-tuple-element.168), kind=kOutput, calls=%fused_computation.clone.1 | convolution fusion | flops 135262208 | bytes 737792 | tf_op jit(solution)/shard_map/while/body/eval_jaxpr/dot_general | solution.py:12
  44.2 0.6 bitcast_dynamic-update-slice_fusion.4
  44.8 1.5 %multiply_reduce_fusion.2 = f32[16,256]{1,0:T(8,128)S(1)} fusion(f32[128,256]{1,0:T(8,128)S(1)} %convert_element_type.9, bf16[16,16,128,128]{3,2,1,0:T(8,128)(2,1)} %get-tuple-element.167, s32[]{:T(128)} %get-tuple-element.159, bf16[128,256]{1,0:T(8,128)(2,1)S(1)} %get-tuple-element.168), kind=kOutput, calls=%fused_computation.clone.1 | convolution fusion | flops 135262208 | bytes 737792 | tf_op jit(solution)/shard_map/while/body/eval_jaxpr/dot_general | solution.py:12
  46.3 0.6 bitcast_dynamic-update-slice_fusion.4
  46.9 1.5 %multiply_reduce_fusion.2 = f32[16,256]{1,0:T(8,128)S(1)} fusion(f32[128,256]{1,0:T(8,128)S(1)} %convert_element_type.9, bf16[16,16,128,128]{3,2,1,0:T(8,128)(2,1)} %get-tuple-element.167, s32[]{:T(128)} %get-tuple-element.159, bf16[128,256]{1,0:T(8,128)(2,1)S(1)} %get-tuple-element.168), kind=kOutput, calls=%fused_computation.clone.1 | convolution fusion | flops 135262208 | bytes 737792 | tf_op jit(solution)/shard_map/while/body/eval_jaxpr/dot_general | solution.py:12
  48.4 0.6 bitcast_dynamic-update-slice_fusion.4
  49.0 1.5 %multiply_reduce_fusion.2 = f32[16,256]{1,0:T(8,128)S(1)} fusion(f32[128,256]{1,0:T(8,128)S(1)} %convert_element_type.9, bf16[16,16,128,128]{3,2,1,0:T(8,128)(2,1)} %get-tuple-element.167, s32[]{:T(128)} %get-tuple-element.159, bf16[128,256]{1,0:T(8,128)(2,1)S(1)} %get-tuple-element.168), kind=kOutput, calls=%fused_computation.clone.1 | convolution fusion | flops 135262208 | bytes 737792 | tf_op jit(solution)/shard_map/while/body/eval_jaxpr/dot_general | solution.py:12
  50.5 0.6 bitcast_dynamic-update-slice_fusion.4
  51.1 1.5 %multiply_reduce_fusion.2 = f32[16,256]{1,0:T(8,128)S(1)} fusion(f32[128,256]{1,0:T(8,128)S(1)} %convert_element_type.9, bf16[16,16,128,128]{3,2,1,0:T(8,128)(2,1)} %get-tuple-element.167, s32[]{:T(128)} %get-tuple-element.159, bf16[128,256]{1,0:T(8,128)(2,1)S(1)} %get-tuple-element.168), kind=kOutput, calls=%fused_computation.clone.1 | convolution fusion | flops 135262208 | bytes 737792 | tf_op jit(solution)/shard_map/while/body/eval_jaxpr/dot_general | solution.py:12
  53.2 1.5 %multiply_reduce_fusion.2 = f32[16,256]{1,0:T(8,128)S(1)} fusion(f32[128,256]{1,0:T(8,128)S(1)} %convert_element_type.9, bf16[16,16,128,128]{3,2,1,0:T(8,128)(2,1)} %get-tuple-element.167, s32[]{:T(128)} %get-tuple-element.159, bf16[128,256]{1,0:T(8,128)(2,1)S(1)} %get-tuple-element.168), kind=kOutput, calls=%fused_computation.clone.1 | convolution fusion | flops 135262208 | bytes 737792 | tf_op jit(solution)/shard_map/while/body/eval_jaxpr/dot_general | solution.py:12
  54.7 0.6 bitcast_dynamic-update-slice_fusion.4
  55.3 1.5 %multiply_reduce_fusion.2 = f32[16,256]{1,0:T(8,128)S(1)} fusion(f32[128,256]{1,0:T(8,128)S(1)} %convert_element_type.9, bf16[16,16,128,128]{3,2,1,0:T(8,128)(2,1)} %get-tuple-element.167, s32[]{:T(128)} %get-tuple-element.159, bf16[128,256]{1,0:T(8,128)(2,1)S(1)} %get-tuple-element.168), kind=kOutput, calls=%fused_computation.clone.1 | convolution fusion | flops 135262208 | bytes 737792 | tf_op jit(solution)/shard_map/while/body/eval_jaxpr/dot_general | solution.py:12
  56.8 0.6 bitcast_dynamic-update-slice_fusion.4
  57.4 1.5 %multiply_reduce_fusion.2 = f32[16,256]{1,0:T(8,128)S(1)} fusion(f32[128,256]{1,0:T(8,128)S(1)} %convert_element_type.9, bf16[16,16,128,128]{3,2,1,0:T(8,128)(2,1)} %get-tuple-element.167, s32[]{:T(128)} %get-tuple-element.159, bf16[128,256]{1,0:T(8,128)(2,1)S(1)} %get-tuple-element.168), kind=kOutput, calls=%fused_computation.clone.1 | convolution fusion | flops 135262208 | bytes 737792 | tf_op jit(solution)/shard_map/while/body/eval_jaxpr/dot_general | solution.py:12
  58.9 0.6 bitcast_dynamic-update-slice_fusion.4
  59.7 2.2 %all-gather = f32[512,256]{1,0:T(8,128)S(1)} all-gather(f32[256,256]{1,0:T(8,128)S(1)} %fusion.17), channel_id=2, replica_groups=mesh['ia'=4,'ja'=4,'ka'=2] {'ka'}, dimensions={0}, use_global_device_ids=true | all-gather | bytes 786432 | tf_op jit(solution)/shard_map/all_gather | solution.py:32
  62.1 1.0 select_add_fusion
  63.3 11.7 %cholesky.49 = f32[128,128]{1,0:T(8,128)S(1)} custom-call(f32[128,128]{1,0:T(8,128)S(1)} %cholesky.115), custom_call_target="Cholesky" | custom-call | tf_op jit(solution)/shard_map/jit(cholesky)/cholesky | solution.py:43
  75.0 9.8 %custom-call.18 = f32[1,128,128]{1,2,0:T(8,128)S(1)} custom-call(f32[1,128,128]{2,1,0:T(8,128)S(1)} %get-tuple-element.75), custom_call_target="InvertDiagBlocksLowerTriangular" | custom-call | tf_op jit(solution)/shard_map/jit(cholesky)/cholesky | solution.py:43
  85.3 11.7 %cholesky.103 = f32[128,128]{1,0:T(8,128)S(1)} custom-call(f32[128,128]{1,0:T(8,128)S(1)} %convolution_subtract_fusion), custom_call_target="Cholesky" | custom-call | tf_op jit(solution)/shard_map/jit(cholesky)/cholesky | solution.py:43
  97.4 0.7 compare_reduce_fusion
  99.5 4.4 %while.12 = (s32[]{:T(128)}, f32[256,256]{0,1:T(8,128)S(1)}, s32[2,2]{1,0:T(2,128)S(1)}, f32[2,128,128]{2,1,0:T(8,128)S(1)}, s32[]{:T(128)}) while((s32[]{:T(128)}, f32[256,256]{0,1:T(8,128)S(1)}, s32[2,2]{1,0:T(2,128)S(1)}, f32[2,128,128]{2,1,0:T(8,128)S(1)}, s32[]{:T(128)}) %tuple.37), condition=%wide.while_cond, body=%wide.while_body.sunk | while | flops 2 | bytes 393321 | solution.py:44
  99.7 0.7 fusion.34
  100.3 1.3 dynamic-slice.7
  101.8 0.7 fusion.34
  102.5 1.3 dynamic-slice.7
  103.9 19.7 %custom-call.19 = f32[2,128,128]{1,2,0:T(8,128)S(1)} custom-call(f32[2,128,128]{2,1,0:T(8,128)S(1)} %get-tuple-element.40), custom_call_target="InvertDiagBlocksLowerTriangular" | custom-call | tf_op jit(solution)/shard_map/jit(_cho_solve)/triangular_solve | solution.py:44
  123.7 0.9 fusion.9
  124.5 0.9 convolution_subtract_fusion.2
  126.4 0.6 maximum_bitcast_fusion
  (57 shorter events, 4.8 us)
Async XLA Ops:
  7.4 54.7 %all-reduce.3.cloned.1.call-start = ((), (), s32[]{:S(2)}) async-start(), calls=%async_computation.1 | async-start | bytes 524288 | tf_op jit(solution)/shard_map/psum | solution.py:30
  10.5 113.1 %reduce-scatter.2.cloned.1.call-start = ((), (), s32[]{:S(2)}) async-start(), calls=%async_computation.2 | async-start | bytes 294912 | tf_op jit(solution)/shard_map/reduce_scatter | solution.py:37
Sparse Core Ops, SparseCore 0:
  10.7 38.3 all-reduce.2
Sparse Core Ops, SparseCore 1:
  59.6 31.8 reduce-scatter.1
